TPU v7x, 32 devices: a whole 2x2x4 slice. The times are simulated.
32 devices in a mesh: seq: 16 (over z, y, x), head: 2 (over core).
Axes of the slice: x: 2, y: 2, z: 4, core: 2. Of those that a mesh axis runs over, the one named last changes fastest.
Arguments:
- queries: bfloat16 [4096, 32, 128], P('seq', 'head'), may hold values from -192 to 192
- keys: bfloat16 [4096, 8, 128], P(('seq', 'head')), may hold values from -6 to 6
- values: bfloat16 [4096, 8, 128], P(('seq', 'head')), may hold values from -6 to 6
- doc_start: int32 [4096], P('seq'), may hold values from 0 to 4095, as said below
- tile_list: int32 [16, 18], P('seq'), may hold values from 0 to 31, as said below
- tile_count: int32 [16], P('seq'), may hold values from 2 to 18, as said below
Outputs:
- attention_out: bfloat16 [4096, 32, 128], P('seq', 'head')
Inputs may be any that keep to these rules, and one draw needn't show every extreme that they name: doc_start never falls, doc_start[i] <= i, and a new document begins at each position where it changes; documents hold 1 to 2048 tokens, one exactly 2048. `tile_list`: row s holds in its first tile_count[s] entries, ascending, exactly the tiles (tile t holds key positions t * 128 to t * 128 + 127) that contain a key visible to some query of positions s * 256 to s * 256 + 255; the later entries equal s * 2. `tile_count`: some row reaches 18.
All inputs are finite; a program needn't handle non-finite values.
Results may differ from a plain program's by a relative error of at most 0.004.
Values may be sent and summed in bfloat16 or wider, within the bound.
No kernel may reach another device: no remote copies, remote signals or barrier semaphores. Data moves between devices by JAX's collectives and lax.ppermute only.
A program may use at most 64 MiB of HBM per device.

v0:
```python
import functools

import jax
import jax.numpy as jnp
from jax import lax
from jax.experimental import pallas as pl
from jax.experimental.pallas import tpu as pltpu
from jax.sharding import PartitionSpec as P


TILE = 128
MAXDOC = 2048
LOG2E = 1.4426950408889634
big_negative = -1e30


def attend_kernel(meta, *refs, blocks, first, last, factor):
    refs = list(refs)
    q_ref, starts_ref, pos_ref = refs[:3]
    block_refs = refs[3 : 3 + blocks]
    refs = refs[3 + blocks :]
    if not first:
        top_in, sum_in, acc_in = refs[:3]
        refs = refs[3:]
    if last:
        out_ref, top_ref, sum_ref, acc_ref, bias_ref = refs
    else:
        top_ref, sum_ref, acc_ref, bias_ref = refs
    group = q_ref.shape[0]
    tokens = q_ref.shape[1]
    tile = block_refs[0].shape[3]
    width = block_refs[0].shape[0] * tile

    if first:
        top_ref[...] = jnp.full(top_ref.shape, big_negative, jnp.float32)
        sum_ref[...] = jnp.zeros(sum_ref.shape, jnp.float32)
        acc_ref[...] = jnp.zeros(acc_ref.shape, jnp.float32)
    else:
        top_ref[...] = top_in[...]
        sum_ref[...] = sum_in[...]
        acc_ref[...] = acc_in[...]

    @pl.when(pl.program_id(0) == 0)
    def _():
        row = lax.broadcasted_iota(jnp.int32, (width, tokens), 0)
        for b in range(blocks):
            key_pos = row + meta[b, 0]
            alive = jnp.where(row < tile, meta[b, 1], meta[b, 2]) > 0
            seen = (key_pos >= starts_ref[...]) & (key_pos <= pos_ref[...]) & alive
            bias_ref[b] = jnp.where(seen, 0.0, big_negative)

    for h in range(group):
        q = q_ref[h]
        top_old = top_ref[0, h : h + 1]
        scores = []
        top_new = top_old
        for blk in block_refs:
            k = blk[:, 0, 0].reshape(width, q.shape[1])
            s = lax.dot_general(
                k, q, (((1,), (1,)), ((), ())), preferred_element_type=jnp.float32
            )
            s = s + bias_ref[len(scores)]
            scores.append(s)
            top_new = jnp.maximum(top_new, jnp.max(s, axis=0, keepdims=True))
        alpha = jnp.exp2((top_old - top_new) * factor)
        top_ref[0, h : h + 1] = top_new
        weight_sum = sum_ref[0, h] * alpha
        acc = acc_ref[h] * alpha
        for blk, s in zip(block_refs, scores):
            p = jnp.exp2((s - top_new) * factor)
            weight_sum = weight_sum + jnp.sum(p.reshape(width // 8, 8, tokens), axis=0)
            v_t = jnp.concatenate([blk[0, 1, 0], blk[1, 1, 0]], axis=1)
            acc = acc + jnp.dot(v_t, p.astype(jnp.bfloat16), preferred_element_type=jnp.float32)
        sum_ref[0, h] = weight_sum
        acc_ref[h] = acc

    if last:
        for h in range(group):
            total = jnp.sum(sum_ref[0, h], axis=0, keepdims=True)
            out_ref[h] = (acc_ref[h] / total).T.astype(jnp.bfloat16)


def attend(q, starts, pos, meta, blocks, state, last):
    heads, tokens, head_dim = q.shape
    key_heads = blocks[0].shape[2]
    group = heads // key_heads
    first = state is None
    n = len(blocks)
    width = blocks[0].shape[0] * blocks[0].shape[3]
    q_spec = pl.BlockSpec((group, tokens, head_dim), lambda g, m: (g, 0, 0))
    row_spec = pl.BlockSpec((1, tokens), lambda g, m: (0, 0))
    bs = blocks[0].shape
    blk_spec = pl.BlockSpec((bs[0], bs[1], 1, bs[3], bs[4]), lambda g, m: (0, 0, g, 0, 0))
    top_spec = pl.BlockSpec((1, group, tokens), lambda g, m: (g, 0, 0))
    sum_spec = pl.BlockSpec((1, group, 8, tokens), lambda g, m: (g, 0, 0, 0))
    acc_spec = pl.BlockSpec((group, head_dim, tokens), lambda g, m: (g, 0, 0))
    state_specs = [top_spec, sum_spec, acc_spec]
    state_shapes = [
        jax.ShapeDtypeStruct((key_heads, group, tokens), jnp.float32),
        jax.ShapeDtypeStruct((key_heads, group, 8, tokens), jnp.float32),
        jax.ShapeDtypeStruct((heads, head_dim, tokens), jnp.float32),
    ]
    scratch = [pltpu.VMEM((n, width, tokens), jnp.float32)]
    if last:
        out_specs = q_spec
        out_shape = jax.ShapeDtypeStruct((heads, tokens, head_dim), jnp.bfloat16)
        scratch = [
            pltpu.VMEM((1, group, tokens), jnp.float32),
            pltpu.VMEM((1, group, 8, tokens), jnp.float32),
            pltpu.VMEM((group, head_dim, tokens), jnp.float32),
        ] + scratch
    else:
        out_specs, out_shape = state_specs, state_shapes
    kernel = functools.partial(
        attend_kernel, blocks=n, first=first, last=last, factor=float(head_dim ** (-0.5) * LOG2E)
    )
    call = pl.pallas_call(
        kernel,
        grid_spec=pltpu.PrefetchScalarGridSpec(
            num_scalar_prefetch=1,
            grid=(key_heads,),
            in_specs=[q_spec, row_spec, row_spec] + [blk_spec] * n + ([] if first else state_specs),
            out_specs=out_specs,
            scratch_shapes=scratch,
        ),
        out_shape=out_shape,
        cost_estimate=pl.CostEstimate(
            flops=4 * n * heads * tokens * width * head_dim, transcendentals=0, bytes_accessed=0
        ),
    )
    return call(meta, q, starts, pos, *blocks, *([] if first else state))


def permuted(x, pairs):
    return lax.ppermute(x, "seq", pairs)


def body(queries, keys, values, doc_start, tile_list, tile_count):
    tokens, _, head_dim = queries.shape
    halves = lax.axis_size("head")
    devices = lax.axis_size("seq")
    key_heads = keys.shape[1] // halves
    own_tokens = keys.shape[0]
    tiles_own = tokens // TILE
    reach_back = MAXDOC // tokens
    side = reach_back // 2
    assert side == 4 and own_tokens == TILE and halves == tiles_own

    k = jnp.transpose(keys, (1, 0, 2)).reshape(halves, key_heads, TILE, head_dim)
    v = jnp.transpose(values, (1, 2, 0)).reshape(halves, key_heads, head_dim, TILE)
    own = lax.all_to_all(jnp.stack([k, v], 1), "head", split_axis=0, concat_axis=0, tiled=True)

    shard = lax.axis_index("seq")
    j = shard % side
    everyone = range(devices)
    ring = {0: 1, 1: 3, 3: 2, 2: 0}
    back = {b: a for a, b in ring.items()}

    def to(step, keep):
        return [(i, i - i % side + step(i % side)) for i in everyone if keep(i % side)]

    onward = [(i, i + side) for i in range(devices - side)]
    z1 = permuted(own, onward)
    up_x = permuted(own, to(lambda c: c ^ 1, lambda c: c < c ^ 1))
    up_y = permuted(own, to(lambda c: c ^ 2, lambda c: c < c ^ 2))
    z2 = permuted(z1, onward)
    x1 = permuted(z1, to(lambda c: c ^ 1, lambda c: True))
    y1 = permuted(z1, to(lambda c: c ^ 2, lambda c: True))
    relay0 = permuted(jnp.where(j == 1, up_x, up_y), to(lambda c: ring[c], lambda c: c in (1, 3)))
    relay1 = permuted(jnp.where((j == 0) | (j == 3), x1, y1), to(lambda c: back[c], lambda c: True))
    down_x = permuted(z2, to(lambda c: c ^ 1, lambda c: c > c ^ 1))
    down_y = permuted(z2, to(lambda c: c ^ 2, lambda c: c > c ^ 2))
    relay2 = permuted(
        jnp.where(j == 0, down_y, down_x), to(lambda c: ring[c], lambda c: c in (0, 2))
    )

    slot_live = jnp.arange(tile_list.shape[1], dtype=jnp.int32) < tile_count[0]
    listed = jnp.where(slot_live, tile_list[0], -1)

    never = jnp.int32(-1)
    one = shard - side
    two = shard - 2 * side
    diagonal = lambda plane: plane - j + (side - 1 - j)
    beside = lambda plane, bit: plane - j + (j ^ bit)
    ids = [
        shard,
        one,
        jnp.where(j > (j ^ 1), beside(shard, 1), never),
        jnp.where(j > (j ^ 2), beside(shard, 2), never),
        two,
        beside(one, 1),
        beside(one, 2),
        jnp.where(j >= 2, diagonal(shard), never),
        diagonal(one),
        jnp.where(j < (j ^ 1), beside(two, 1), never),
        jnp.where(j < (j ^ 2), beside(two, 2), never),
        jnp.where(j < 2, diagonal(two), never),
    ]
    ids = jnp.stack(ids)
    tiles = ids[:, None] * tiles_own + jnp.arange(tiles_own, dtype=jnp.int32)[None, :]
    live = jnp.any(tiles[:, :, None] == listed[None, None, :], axis=2) & (ids[:, None] >= 0)
    meta = jnp.concatenate([ids[:, None] * tokens, live.astype(jnp.int32)], axis=1)

    q = jnp.transpose(queries, (1, 0, 2))
    starts = doc_start.reshape(1, tokens)
    pos = (shard * tokens + jnp.arange(tokens, dtype=jnp.int32)).reshape(1, tokens)
    groups = [
        [own, z1, up_x, up_y],
        [z2, x1, y1, relay0],
        [relay1, down_x, down_y, relay2],
    ]
    state = None
    at = 0
    for n, blocks in enumerate(groups):
        state = attend(
            q, starts, pos, meta[at : at + len(blocks)], blocks, state, n == len(groups) - 1
        )
        at += len(blocks)
    return jnp.transpose(state, (1, 0, 2))


def solution(mesh):
    in_specs = (
        P("seq", "head", None),
        P(("seq", "head"), None, None),
        P(("seq", "head"), None, None),
        P("seq"),
        P("seq", None),
        P("seq"),
    )
    out_specs = P("seq", "head", None)
    return jax.shard_map(body, mesh=mesh, in_specs=in_specs, out_specs=out_specs, check_vma=False)
```

profile of v0, /device:TPU:0, one launch (start us, length us, event | category | flops | bytes accessed | tf_op | source)
XLA Modules:
  0.0 106.5 jit_solution(169934194774539997)
XLA Ops:
  0.0 1.0 copy.20
  1.0 1.2 %copy.21 = bf16[8,128,128]{2,1,0:T(8,128)(2,1)S(1)} copy(bf16[8,128,128]{1,0,2:T(8,128)(2,1)} %bitcast.44) | data formatting | bytes 524288 | tf_op jit(solution)/shard_map/transpose | solution.py:150
  2.2 4.2 %all_to_all.5.refs_3_ = bf16[2,2,4,128,128]{4,3,2,1,0:T(8,128)(2,1)S(1)} all-to-all(bf16[2,2,4,128,128]{4,3,2,1,0:T(8,128)(2,1)S(1)} %pad_maximum_fusion), channel_id=1, replica_groups=mesh['seq'=16,'head'=2] {'head'}, dimensions={0} | all-to-all | bytes 1048576 | tf_op jit(solution)/shard_map/all_to_all | solution.py:151
  6.4 5.8 %collective-permute-start = (bf16[2,2,4,128,128]{4,3,2,1,0:T(8,128)(2,1)S(1)}, bf16[2,2,4,128,128]{4,3,2,1,0:T(8,128)(2,1)}, u32[]{:S(2)}, u32[]{:S(2)}) collective-permute-start(bf16[2,2,4,128,128]{4,3,2,1,0:T(8,128)(2,1)S(1)} %all_to_all.5.refs_3_), channel_id=1, source_target_pairs={{0,8},{2,10},{4,12},{6,14},{8,16},{10,18},{12,20},{14,22},{16,24},... | collective-permute-start | bytes 1572872 | tf_op jit(solution)/shard_map/ppermute | solution.py:135
  12.1 3.4 %collective-permute-start.8 = (bf16[2,2,4,128,128]{4,3,2,1,0:T(8,128)(2,1)S(1)}, bf16[2,2,4,128,128]{4,3,2,1,0:T(8,128)(2,1)S(1)}, u32[]{:S(2)}, u32[]{:S(2)}) collective-permute-start(bf16[2,2,4,128,128]{4,3,2,1,0:T(8,128)(2,1)S(1)} %all_to_all.5.refs_3_), channel_id=1, source_target_pairs={{0,2},{4,6},{8,10},{12,14},{16,18},{20,22},{24,26},{28,30},{1,3},{... | collective-permute-start | bytes 1572872 | tf_op jit(solution)/shard_map/ppermute | solution.py:135
  15.6 3.5 %collective-permute-start.9 = (bf16[2,2,4,128,128]{4,3,2,1,0:T(8,128)(2,1)S(1)}, bf16[2,2,4,128,128]{4,3,2,1,0:T(8,128)(2,1)S(1)}, u32[]{:S(2)}, u32[]{:S(2)}) collective-permute-start(bf16[2,2,4,128,128]{4,3,2,1,0:T(8,128)(2,1)S(1)} %all_to_all.5.refs_3_), channel_id=1, source_target_pairs={{0,4},{2,6},{8,12},{10,14},{16,20},{18,22},{24,28},{26,30},{1,5},{... | collective-permute-start | bytes 1572872 | tf_op jit(solution)/shard_map/ppermute | solution.py:135
  19.1 0.1 stack.93
  19.8 0.1 stack.80
  20.0 0.2 compare_reduce_fusion
  20.2 2.6 %collective-permute-done.refs_4_ = bf16[2,2,4,128,128]{4,3,2,1,0:T(8,128)(2,1)} collective-permute-done((bf16[2,2,4,128,128]{4,3,2,1,0:T(8,128)(2,1)S(1)}, bf16[2,2,4,128,128]{4,3,2,1,0:T(8,128)(2,1)}, u32[]{:S(2)}, u32[]{:S(2)}) %collective-permute-start) | collective-permute-done | bytes 524320 | tf_op jit(solution)/shard_map/ppermute | solution.py:135
  22.8 4.5 %collective-permute-start.4 = (bf16[2,2,4,128,128]{4,3,2,1,0:T(8,128)(2,1)}, bf16[2,2,4,128,128]{4,3,2,1,0:T(8,128)(2,1)S(1)}, u32[]{:S(2)}, u32[]{:S(2)}) collective-permute-start(bf16[2,2,4,128,128]{4,3,2,1,0:T(8,128)(2,1)} %collective-permute-done.refs_4_), channel_id=1, source_target_pairs={{0,8},{2,10},{4,12},{6,14},{8,16},{10,18},{12,20},{14,22},{16,24},... | collective-permute-start | bytes 1572872 | tf_op jit(solution)/shard_map/ppermute | solution.py:135
  27.3 1.6 %collective-permute-start.1 = (bf16[2,2,4,128,128]{4,3,2,1,0:T(8,128)(2,1)}, bf16[2,2,4,128,128]{4,3,2,1,0:T(8,128)(2,1)S(1)}, u32[]{:S(2)}, u32[]{:S(2)}) collective-permute-start(bf16[2,2,4,128,128]{4,3,2,1,0:T(8,128)(2,1)} %collective-permute-done.refs_4_), channel_id=1, source_target_pairs={{0,2},{2,0},{4,6},{6,4},{8,10},{10,8},{12,14},{14,12},{16,18},{18,... | collective-permute-start | bytes 1572872 | tf_op jit(solution)/shard_map/ppermute | solution.py:135
  28.9 1.5 %collective-permute-start.2 = (bf16[2,2,4,128,128]{4,3,2,1,0:T(8,128)(2,1)}, bf16[2,2,4,128,128]{4,3,2,1,0:T(8,128)(2,1)S(1)}, u32[]{:S(2)}, u32[]{:S(2)}) collective-permute-start(bf16[2,2,4,128,128]{4,3,2,1,0:T(8,128)(2,1)} %collective-permute-done.refs_4_), channel_id=1, source_target_pairs={{0,4},{2,6},{4,0},{6,2},{8,12},{10,14},{12,8},{14,10},{16,20},{18,... | collective-permute-start | bytes 1572872 | tf_op jit(solution)/shard_map/ppermute | solution.py:135
  30.4 7.8 %collective-permute-done.4.refs_3_ = bf16[2,2,4,128,128]{4,3,2,1,0:T(8,128)(2,1)S(1)} collective-permute-done((bf16[2,2,4,128,128]{4,3,2,1,0:T(8,128)(2,1)}, bf16[2,2,4,128,128]{4,3,2,1,0:T(8,128)(2,1)S(1)}, u32[]{:S(2)}, u32[]{:S(2)}) %collective-permute-start.4) | collective-permute-done | bytes 524320 | tf_op jit(solution)/shard_map/ppermute | solution.py:135
  38.2 1.3 %collective-permute-start.5 = (bf16[2,2,4,128,128]{4,3,2,1,0:T(8,128)(2,1)S(1)}, bf16[2,2,4,128,128]{4,3,2,1,0:T(8,128)(2,1)S(1)}, u32[]{:S(2)}, u32[]{:S(2)}) collective-permute-start(bf16[2,2,4,128,128]{4,3,2,1,0:T(8,128)(2,1)S(1)} %collective-permute-done.4.refs_3_), channel_id=1, source_target_pairs={{2,0},{6,4},{10,8},{14,12},{18,16},{22,20},{26,24},{30,28},{3,1},{... | collective-permute-start | bytes 1572872 | tf_op jit(solution)/shard_map/ppermute | solution.py:135
  39.5 1.3 %collective-permute-start.6 = (bf16[2,2,4,128,128]{4,3,2,1,0:T(8,128)(2,1)S(1)}, bf16[2,2,4,128,128]{4,3,2,1,0:T(8,128)(2,1)S(1)}, u32[]{:S(2)}, u32[]{:S(2)}) collective-permute-start(bf16[2,2,4,128,128]{4,3,2,1,0:T(8,128)(2,1)S(1)} %collective-permute-done.4.refs_3_), channel_id=1, source_target_pairs={{4,0},{6,2},{12,8},{14,10},{20,16},{22,18},{28,24},{30,26},{5,1},{... | collective-permute-start | bytes 1572872 | tf_op jit(solution)/shard_map/ppermute | solution.py:135
  40.8 0.9 broadcast_select_fusion
  41.8 1.5 %collective-permute-start.10 = (bf16[2,2,4,128,128]{4,3,2,1,0:T(8,128)(2,1)}, bf16[2,2,4,128,128]{4,3,2,1,0:T(8,128)(2,1)}, u32[]{:S(2)}, u32[]{:S(2)}) collective-permute-start(bf16[2,2,4,128,128]{4,3,2,1,0:T(8,128)(2,1)} %broadcast_select_fusion), channel_id=1, source_target_pairs={{2,6},{6,4},{10,14},{14,12},{18,22},{22,20},{26,30},{30,28},{3,7},... | collective-permute-start | bytes 1572872 | tf_op jit(solution)/shard_map/ppermute | solution.py:135
  43.3 0.9 broadcast_select_fusion.2
  44.2 2.5 %collective-permute-start.3 = (bf16[2,2,4,128,128]{4,3,2,1,0:T(8,128)(2,1)}, bf16[2,2,4,128,128]{4,3,2,1,0:T(8,128)(2,1)}, u32[]{:S(2)}, u32[]{:S(2)}) collective-permute-start(bf16[2,2,4,128,128]{4,3,2,1,0:T(8,128)(2,1)} %broadcast_select_fusion.2), channel_id=1, source_target_pairs={{0,4},{2,0},{4,6},{6,2},{8,12},{10,8},{12,14},{14,10},{16,20},{18,... | collective-permute-start | bytes 1572872 | tf_op jit(solution)/shard_map/ppermute | solution.py:135
  46.7 8.2 %collective-permute-done.5.refs_4_ = bf16[2,2,4,128,128]{4,3,2,1,0:T(8,128)(2,1)S(1)} collective-permute-done((bf16[2,2,4,128,128]{4,3,2,1,0:T(8,128)(2,1)S(1)}, bf16[2,2,4,128,128]{4,3,2,1,0:T(8,128)(2,1)S(1)}, u32[]{:S(2)}, u32[]{:S(2)}) %collective-permute-start.5) | collective-permute-done | bytes 524320 | tf_op jit(solution)/shard_map/ppermute | solution.py:135
  54.9 0.9 broadcast_select_fusion.1
  55.8 5.9 %collective-permute-start.7 = (bf16[2,2,4,128,128]{4,3,2,1,0:T(8,128)(2,1)}, bf16[2,2,4,128,128]{4,3,2,1,0:T(8,128)(2,1)}, u32[]{:S(2)}, u32[]{:S(2)}) collective-permute-start(bf16[2,2,4,128,128]{4,3,2,1,0:T(8,128)(2,1)} %broadcast_select_fusion.1), channel_id=1, source_target_pairs={{0,2},{4,0},{8,10},{12,8},{16,18},{20,16},{24,26},{28,24},{1,3},{5... | collective-permute-start | bytes 1572872 | tf_op jit(solution)/shard_map/ppermute | solution.py:135
  61.8 0.6 copy.27.meta
  62.4 1.2 %copy.29 = bf16[256,16,128]{2,0,1:T(8,128)(2,1)} copy(bf16[256,16,128]{2,1,0:T(8,128)(2,1)S(1)} %copy-done) | data formatting | bytes 2097152 | tf_op args[0]
  63.7 0.7 copy.26.meta
  64.3 0.7 copy.25.meta
  65.0 0.6 iota_add_fusion.refs_2_
  65.6 12.1 %shard_map.64 = (f32[4,4,256]{2,1,0:T(4,128)}, f32[4,4,8,256]{3,2,1,0:T(8,128)}, f32[16,128,256]{2,1,0:T(8,128)}) custom-call(s32[4,3]{1,0:T(4,128)} %copy.27.meta, bf16[16,256,128]{2,1,0:T(8,128)(2,1)} %bitcast.37, s32[1,256]{1,0:T(1,128)} %bitcast.45, s32[1,256]{1,0:T(1,128)} %iota_add_fusion.refs_2_, bf16[2,2,4,128,128]{4,3,2,1,0:T(8,128)(2,1)} %copy-done.1, ...), custom_call_target="tpu_custom_call" | custom-call | flops 2147483648 | tf_op jit(solution)/shard_map/pallas_call | solution.py:131
  77.7 12.4 %shard_map.65 = (f32[4,4,256]{2,1,0:T(4,128)}, f32[4,4,8,256]{3,2,1,0:T(8,128)}, f32[16,128,256]{2,1,0:T(8,128)}) custom-call(s32[4,3]{1,0:T(4,128)} %copy.26.meta, bf16[16,256,128]{2,1,0:T(8,128)(2,1)} %bitcast.38, s32[1,256]{1,0:T(1,128)} %bitcast.46, s32[1,256]{1,0:T(1,128)} %iota_add_fusion.refs_2_, bf16[2,2,4,128,128]{4,3,2,1,0:T(8,128)(2,1)} %copy-done.8, ...), custom_call_target="tpu_custom_call" | custom-call | flops 2147483648 | tf_op jit(solution)/shard_map/pallas_call | solution.py:131
  90.2 13.4 %shard_map.66 = bf16[16,256,128]{2,1,0:T(8,128)(2,1)} custom-call(s32[4,3]{1,0:T(4,128)} %copy.25.meta, bf16[16,256,128]{2,1,0:T(8,128)(2,1)} %bitcast.39, s32[1,256]{1,0:T(1,128)} %bitcast.47, s32[1,256]{1,0:T(1,128)} %iota_add_fusion.refs_2_, bf16[2,2,4,128,128]{4,3,2,1,0:T(8,128)(2,1)} %collective-permute-done.3.refs_3_, ...), custom_call_target="tpu_custom_call" | custom-call | flops 2147483648 | tf_op jit(solution)/shard_map/pallas_call | solution.py:131
  103.6 2.9 %copy.24 = bf16[256,16,128]{2,1,0:T(8,128)(2,1)} copy(bf16[256,16,128]{2,0,1:T(8,128)(2,1)} %bitcast.40) | data formatting | bytes 2097152 | tf_op jit(solution)/shard_map/transpose | solution.py:219
  (37 shorter events, 0.2 us)
Async XLA Ops:
  0.0 20.0 %copy-start.9 = (s32[1,18]{1,0:T(1,128)S(1)}, s32[1,18]{1,0:T(1,128)}, u32[]{:S(2)}) copy-start(s32[1,18]{1,0:T(1,128)} %param.10) | copy-start | bytes 220
  6.4 49.4 %copy-start.1 = (bf16[2,2,4,128,128]{4,3,2,1,0:T(8,128)(2,1)}, bf16[2,2,4,128,128]{4,3,2,1,0:T(8,128)(2,1)S(1)}, u32[]{:S(2)}) copy-start(bf16[2,2,4,128,128]{4,3,2,1,0:T(8,128)(2,1)S(1)} %all_to_all.5.refs_3_) | copy-start | bytes 1572868
  6.4 16.4 %collective-permute-start = (bf16[2,2,4,128,128]{4,3,2,1,0:T(8,128)(2,1)S(1)}, bf16[2,2,4,128,128]{4,3,2,1,0:T(8,128)(2,1)}, u32[]{:S(2)}, u32[]{:S(2)}) collective-permute-start(bf16[2,2,4,128,128]{4,3,2,1,0:T(8,128)(2,1)S(1)} %all_to_all.5.refs_3_), channel_id=1, source_target_pairs={{0,8},{2,10},{4,12},{6,14},{8,16},{10,18},{12,20},{14,22},{16,24},... | collective-permute-start | bytes 1572872 | tf_op jit(solution)/shard_map/ppermute | solution.py:135
  12.1 27.4 %collective-permute-start.8 = (bf16[2,2,4,128,128]{4,3,2,1,0:T(8,128)(2,1)S(1)}, bf16[2,2,4,128,128]{4,3,2,1,0:T(8,128)(2,1)S(1)}, u32[]{:S(2)}, u32[]{:S(2)}) collective-permute-start(bf16[2,2,4,128,128]{4,3,2,1,0:T(8,128)(2,1)S(1)} %all_to_all.5.refs_3_), channel_id=1, source_target_pairs={{0,2},{4,6},{8,10},{12,14},{16,18},{20,22},{24,26},{28,30},{1,3},{... | collective-permute-start | bytes 1572872 | tf_op jit(solution)/shard_map/ppermute | solution.py:135
  15.6 25.3 %collective-permute-start.9 = (bf16[2,2,4,128,128]{4,3,2,1,0:T(8,128)(2,1)S(1)}, bf16[2,2,4,128,128]{4,3,2,1,0:T(8,128)(2,1)S(1)}, u32[]{:S(2)}, u32[]{:S(2)}) collective-permute-start(bf16[2,2,4,128,128]{4,3,2,1,0:T(8,128)(2,1)S(1)} %all_to_all.5.refs_3_), channel_id=1, source_target_pairs={{0,4},{2,6},{8,12},{10,14},{16,20},{18,22},{24,28},{26,30},{1,5},{... | collective-permute-start | bytes 1572872 | tf_op jit(solution)/shard_map/ppermute | solution.py:135
  22.8 15.4 %collective-permute-start.4 = (bf16[2,2,4,128,128]{4,3,2,1,0:T(8,128)(2,1)}, bf16[2,2,4,128,128]{4,3,2,1,0:T(8,128)(2,1)S(1)}, u32[]{:S(2)}, u32[]{:S(2)}) collective-permute-start(bf16[2,2,4,128,128]{4,3,2,1,0:T(8,128)(2,1)} %collective-permute-done.refs_4_), channel_id=1, source_target_pairs={{0,8},{2,10},{4,12},{6,14},{8,16},{10,18},{12,20},{14,22},{16,24},... | collective-permute-start | bytes 1572872 | tf_op jit(solution)/shard_map/ppermute | solution.py:135
  27.3 15.9 %collective-permute-start.1 = (bf16[2,2,4,128,128]{4,3,2,1,0:T(8,128)(2,1)}, bf16[2,2,4,128,128]{4,3,2,1,0:T(8,128)(2,1)S(1)}, u32[]{:S(2)}, u32[]{:S(2)}) collective-permute-start(bf16[2,2,4,128,128]{4,3,2,1,0:T(8,128)(2,1)} %collective-permute-done.refs_4_), channel_id=1, source_target_pairs={{0,2},{2,0},{4,6},{6,4},{8,10},{10,8},{12,14},{14,12},{16,18},{18,... | collective-permute-start | bytes 1572872 | tf_op jit(solution)/shard_map/ppermute | solution.py:135
  28.9 14.4 %collective-permute-start.2 = (bf16[2,2,4,128,128]{4,3,2,1,0:T(8,128)(2,1)}, bf16[2,2,4,128,128]{4,3,2,1,0:T(8,128)(2,1)S(1)}, u32[]{:S(2)}, u32[]{:S(2)}) collective-permute-start(bf16[2,2,4,128,128]{4,3,2,1,0:T(8,128)(2,1)} %collective-permute-done.refs_4_), channel_id=1, source_target_pairs={{0,4},{2,6},{4,0},{6,2},{8,12},{10,14},{12,8},{14,10},{16,20},{18,... | collective-permute-start | bytes 1572872 | tf_op jit(solution)/shard_map/ppermute | solution.py:135
  30.4 32.0 %copy-start = (bf16[256,16,128]{2,1,0:T(8,128)(2,1)S(1)}, bf16[256,16,128]{2,1,0:T(8,128)(2,1)}, u32[]{:S(2)}) copy-start(bf16[256,16,128]{2,1,0:T(8,128)(2,1)} %param.6) | copy-start | bytes 3145732
  38.2 17.6 %copy-start.8 = (bf16[2,2,4,128,128]{4,3,2,1,0:T(8,128)(2,1)}, bf16[2,2,4,128,128]{4,3,2,1,0:T(8,128)(2,1)S(1)}, u32[]{:S(2)}) copy-start(bf16[2,2,4,128,128]{4,3,2,1,0:T(8,128)(2,1)S(1)} %collective-permute-done.4.refs_3_) | copy-start | bytes 1572868
  38.2 16.7 %collective-permute-start.5 = (bf16[2,2,4,128,128]{4,3,2,1,0:T(8,128)(2,1)S(1)}, bf16[2,2,4,128,128]{4,3,2,1,0:T(8,128)(2,1)S(1)}, u32[]{:S(2)}, u32[]{:S(2)}) collective-permute-start(bf16[2,2,4,128,128]{4,3,2,1,0:T(8,128)(2,1)S(1)} %collective-permute-done.4.refs_3_), channel_id=1, source_target_pairs={{2,0},{6,4},{10,8},{14,12},{18,16},{22,20},{26,24},{30,28},{3,1},{... | collective-permute-start | bytes 1572872 | tf_op jit(solution)/shard_map/ppermute | solution.py:135
  39.5 16.3 %copy-start.2 = (bf16[2,2,4,128,128]{4,3,2,1,0:T(8,128)(2,1)}, bf16[2,2,4,128,128]{4,3,2,1,0:T(8,128)(2,1)S(1)}, u32[]{:S(2)}) copy-start(bf16[2,2,4,128,128]{4,3,2,1,0:T(8,128)(2,1)S(1)} %collective-permute-done.8.refs_5_) | copy-start | bytes 1572868
  39.5 15.4 %collective-permute-start.6 = (bf16[2,2,4,128,128]{4,3,2,1,0:T(8,128)(2,1)S(1)}, bf16[2,2,4,128,128]{4,3,2,1,0:T(8,128)(2,1)S(1)}, u32[]{:S(2)}, u32[]{:S(2)}) collective-permute-start(bf16[2,2,4,128,128]{4,3,2,1,0:T(8,128)(2,1)S(1)} %collective-permute-done.4.refs_3_), channel_id=1, source_target_pairs={{4,0},{6,2},{12,8},{14,10},{20,16},{22,18},{28,24},{30,26},{5,1},{... | collective-permute-start | bytes 1572872 | tf_op jit(solution)/shard_map/ppermute | solution.py:135
  40.8 15.0 %copy-start.3 = (bf16[2,2,4,128,128]{4,3,2,1,0:T(8,128)(2,1)}, bf16[2,2,4,128,128]{4,3,2,1,0:T(8,128)(2,1)S(1)}, u32[]{:S(2)}) copy-start(bf16[2,2,4,128,128]{4,3,2,1,0:T(8,128)(2,1)S(1)} %collective-permute-done.9.refs_6_) | copy-start | bytes 1572868
  41.8 36.0 %collective-permute-start.10 = (bf16[2,2,4,128,128]{4,3,2,1,0:T(8,128)(2,1)}, bf16[2,2,4,128,128]{4,3,2,1,0:T(8,128)(2,1)}, u32[]{:S(2)}, u32[]{:S(2)}) collective-permute-start(bf16[2,2,4,128,128]{4,3,2,1,0:T(8,128)(2,1)} %broadcast_select_fusion), channel_id=1, source_target_pairs={{2,6},{6,4},{10,14},{14,12},{18,22},{22,20},{26,30},{30,28},{3,7},... | collective-permute-start | bytes 1572872 | tf_op jit(solution)/shard_map/ppermute | solution.py:135
  43.2 18.5 %copy-start.5 = (bf16[2,2,4,128,128]{4,3,2,1,0:T(8,128)(2,1)}, bf16[2,2,4,128,128]{4,3,2,1,0:T(8,128)(2,1)S(1)}, u32[]{:S(2)}) copy-start(bf16[2,2,4,128,128]{4,3,2,1,0:T(8,128)(2,1)S(1)} %collective-permute-done.1.refs_4_) | copy-start | bytes 1572868
  43.3 18.6 %copy-start.6 = (bf16[2,2,4,128,128]{4,3,2,1,0:T(8,128)(2,1)}, bf16[2,2,4,128,128]{4,3,2,1,0:T(8,128)(2,1)S(1)}, u32[]{:S(2)}) copy-start(bf16[2,2,4,128,128]{4,3,2,1,0:T(8,128)(2,1)S(1)} %collective-permute-done.2.refs_5_) | copy-start | bytes 1572868
  44.2 45.9 %collective-permute-start.3 = (bf16[2,2,4,128,128]{4,3,2,1,0:T(8,128)(2,1)}, bf16[2,2,4,128,128]{4,3,2,1,0:T(8,128)(2,1)}, u32[]{:S(2)}, u32[]{:S(2)}) collective-permute-start(bf16[2,2,4,128,128]{4,3,2,1,0:T(8,128)(2,1)} %broadcast_select_fusion.2), channel_id=1, source_target_pairs={{0,4},{2,0},{4,6},{6,2},{8,12},{10,8},{12,14},{14,10},{16,20},{18,... | collective-permute-start | bytes 1572872 | tf_op jit(solution)/shard_map/ppermute | solution.py:135
  54.9 22.8 %copy-start.4 = (bf16[2,2,4,128,128]{4,3,2,1,0:T(8,128)(2,1)}, bf16[2,2,4,128,128]{4,3,2,1,0:T(8,128)(2,1)S(1)}, u32[]{:S(2)}) copy-start(bf16[2,2,4,128,128]{4,3,2,1,0:T(8,128)(2,1)S(1)} %collective-permute-done.5.refs_4_) | copy-start | bytes 1572868
  54.9 6.9 %copy-start.7 = (bf16[2,2,4,128,128]{4,3,2,1,0:T(8,128)(2,1)}, bf16[2,2,4,128,128]{4,3,2,1,0:T(8,128)(2,1)S(1)}, u32[]{:S(2)}) copy-start(bf16[2,2,4,128,128]{4,3,2,1,0:T(8,128)(2,1)S(1)} %collective-permute-done.6.refs_5_) | copy-start | bytes 1572868
  55.8 34.3 %collective-permute-start.7 = (bf16[2,2,4,128,128]{4,3,2,1,0:T(8,128)(2,1)}, bf16[2,2,4,128,128]{4,3,2,1,0:T(8,128)(2,1)}, u32[]{:S(2)}, u32[]{:S(2)}) collective-permute-start(bf16[2,2,4,128,128]{4,3,2,1,0:T(8,128)(2,1)} %broadcast_select_fusion.1), channel_id=1, source_target_pairs={{0,2},{4,0},{8,10},{12,8},{16,18},{20,16},{24,26},{28,24},{1,3},{5... | collective-permute-start | bytes 1572872 | tf_op jit(solution)/shard_map/ppermute | solution.py:135
where the time goes:
time: 107 us; the launch traced here: 106 us
  Pallas kernels  38 us (36%)
  starting transfers between devices  32.7 us (31%)
  waiting for transfers between devices  18.6 us (17%)
  local copies, waits for them, and re-layouts  8.53 us (8%)
  blocking collectives  4.15 us (4%)
  other arithmetic  3.64 us (3%)
    pallas_call x3, Pallas kernels, attend(): return call(meta, q, starts, pos, *blocks, *([] if first else state))  38 us
    ppermute x11, starting transfers between devices, permuted(): return lax.ppermute(x, 'seq', pairs)  32.7 us
    ppermute x11, waiting for transfers between devices, permuted(): return lax.ppermute(x, 'seq', pairs)  18.6 us
    all_to_all x1, blocking collectives, body(): lax.all_to_all(jnp.stack([k, v], 1), 'head', split_axis=0, concat_axis=0,...  4.15 us
    unnamed x24, local copies, waits for them, and re-layouts  3.23 us
    transpose x1, local copies, waits for them, and re-layouts, body(): return jnp.transpose(state, (1, 0, 2))  2.87 us
  transfers between devices with their start and end apart: 11, of which 3 were waited for; matrix products, arithmetic and copies ran while one was open for 7% of the time, Pallas kernels for 23%

commit v1 on v0

--- a/solution.py
+++ b/solution.py
@@ -14,7 +14,7 @@
 big_negative = -1e30
 
 
-def attend_kernel(meta, *refs, blocks, first, last, factor):
+def attend_kernel(meta, *refs, blocks, first, last, factor, at):
     refs = list(refs)
     q_ref, starts_ref, pos_ref = refs[:3]
     block_refs = refs[3 : 3 + blocks]
@@ -44,8 +44,8 @@
     def _():
         row = lax.broadcasted_iota(jnp.int32, (width, tokens), 0)
         for b in range(blocks):
-            key_pos = row + meta[b, 0]
-            alive = jnp.where(row < tile, meta[b, 1], meta[b, 2]) > 0
+            key_pos = row + meta[at + b, 0]
+            alive = jnp.where(row < tile, meta[at + b, 1], meta[at + b, 2]) > 0
             seen = (key_pos >= starts_ref[...]) & (key_pos <= pos_ref[...]) & alive
             bias_ref[b] = jnp.where(seen, 0.0, big_negative)
 
@@ -80,7 +80,7 @@
             out_ref[h] = (acc_ref[h] / total).T.astype(jnp.bfloat16)
 
 
-def attend(q, starts, pos, meta, blocks, state, last):
+def attend(q, starts, pos, meta, blocks, state, last, at=0):
     heads, tokens, head_dim = q.shape
     key_heads = blocks[0].shape[2]
     group = heads // key_heads
@@ -112,7 +112,12 @@
     else:
         out_specs, out_shape = state_specs, state_shapes
     kernel = functools.partial(
-        attend_kernel, blocks=n, first=first, last=last, factor=float(head_dim ** (-0.5) * LOG2E)
+        attend_kernel,
+        blocks=n,
+        first=first,
+        last=last,
+        factor=float(head_dim ** (-0.5) * LOG2E),
+        at=at,
     )
     call = pl.pallas_call(
         kernel,
@@ -191,9 +196,9 @@
         beside(one, 1),
         beside(one, 2),
         jnp.where(j >= 2, diagonal(shard), never),
-        diagonal(one),
         jnp.where(j < (j ^ 1), beside(two, 1), never),
         jnp.where(j < (j ^ 2), beside(two, 2), never),
+        diagonal(one),
         jnp.where(j < 2, diagonal(two), never),
     ]
     ids = jnp.stack(ids)
@@ -206,14 +211,14 @@
     pos = (shard * tokens + jnp.arange(tokens, dtype=jnp.int32)).reshape(1, tokens)
     groups = [
         [own, z1, up_x, up_y],
-        [z2, x1, y1, relay0],
-        [relay1, down_x, down_y, relay2],
+        [z2, x1, y1, relay0, down_x, down_y],
+        [relay1, relay2],
     ]
     state = None
     at = 0
     for n, blocks in enumerate(groups):
         state = attend(
-            q, starts, pos, meta[at : at + len(blocks)], blocks, state, n == len(groups) - 1
+            q, starts, pos, meta, blocks, state, n == len(groups) - 1, at
         )
         at += len(blocks)
     return jnp.transpose(state, (1, 0, 2))

time: 107 us -> 106 us (level)
  starting transfers between devices: 32.7 us -> 28.9 us
  Pallas kernels: 38 us -> 39.4 us
  waiting for transfers between devices: 18.6 us -> 19.8 us
    ppermute x11, starting transfers between devices: 32.7 us -> 28.9 us  [permuted(): return lax.ppermute(x, 'seq', pairs)]
    pallas_call x3, Pallas kernels: 38 us -> 39.4 us  [attend(): return call(meta, q, starts, pos, *blocks, *([] if first else state))]
    ppermute x11, waiting for transfers between devices: 18.6 us -> 19.8 us  [permuted(): return lax.ppermute(x, 'seq', pairs)]
    unnamed x24 -> x25, local copies, waits for them, and re-layouts: 3.23 us -> 2.23 us
  transfers between devices with their start and end apart: 11 -> 11, of which waited for: 3 -> 4; matrix products, arithmetic and copies ran while one was open for 7% -> 6% of each run, Pallas kernels for 23% -> 28%
where the time goes in v1:
time: 106 us; the launch traced here: 105 us
  Pallas kernels  39.4 us (37%)
  starting transfers between devices  28.9 us (27%)
  waiting for transfers between devices  19.8 us (19%)
  local copies, waits for them, and re-layouts  8.13 us (8%)
  blocking collectives  4.15 us (4%)
  other arithmetic  3.75 us (4%)
    pallas_call x3, Pallas kernels, attend(): return call(meta, q, starts, pos, *blocks, *([] if first else state))  39.4 us
    ppermute x11, starting transfers between devices, permuted(): return lax.ppermute(x, 'seq', pairs)  28.9 us
    ppermute x11, waiting for transfers between devices, permuted(): return lax.ppermute(x, 'seq', pairs)  19.8 us
    all_to_all x1, blocking collectives, body(): lax.all_to_all(jnp.stack([k, v], 1), 'head', split_axis=0, concat_axis=0,...  4.15 us
    transpose x1, local copies, waits for them, and re-layouts, body(): return jnp.transpose(state, (1, 0, 2))  2.87 us
    unnamed x25, local copies, waits for them, and re-layouts  2.23 us
  transfers between devices with their start and end apart: 11, of which 4 were waited for; matrix products, arithmetic and copies ran while one was open for 6% of the time, Pallas kernels for 28%

profile of v1, /device:TPU:0, one launch (start us, length us, event | category | flops | bytes accessed | tf_op | source)
XLA Modules:
  0.0 105.1 jit_solution(16760130228450097860)
XLA Ops:
  0.0 1.0 copy.19
  1.0 1.2 %copy.20 = bf16[8,128,128]{2,1,0:T(8,128)(2,1)S(1)} copy(bf16[8,128,128]{1,0,2:T(8,128)(2,1)} %bitcast.44) | data formatting | bytes 524288 | tf_op jit(solution)/shard_map/transpose | solution.py:155
  2.2 4.2 %all_to_all.5.refs_3_ = bf16[2,2,4,128,128]{4,3,2,1,0:T(8,128)(2,1)S(1)} all-to-all(bf16[2,2,4,128,128]{4,3,2,1,0:T(8,128)(2,1)S(1)} %pad_maximum_fusion), channel_id=1, replica_groups=mesh['seq'=16,'head'=2] {'head'}, dimensions={0} | all-to-all | bytes 1048576 | tf_op jit(solution)/shard_map/all_to_all | solution.py:156
  6.4 5.8 %collective-permute-start = (bf16[2,2,4,128,128]{4,3,2,1,0:T(8,128)(2,1)S(1)}, bf16[2,2,4,128,128]{4,3,2,1,0:T(8,128)(2,1)}, u32[]{:S(2)}, u32[]{:S(2)}) collective-permute-start(bf16[2,2,4,128,128]{4,3,2,1,0:T(8,128)(2,1)S(1)} %all_to_all.5.refs_3_), channel_id=1, source_target_pairs={{0,8},{2,10},{4,12},{6,14},{8,16},{10,18},{12,20},{14,22},{16,24},... | collective-permute-start | bytes 1572872 | tf_op jit(solution)/shard_map/ppermute | solution.py:140
  12.1 3.4 %collective-permute-start.8 = (bf16[2,2,4,128,128]{4,3,2,1,0:T(8,128)(2,1)S(1)}, bf16[2,2,4,128,128]{4,3,2,1,0:T(8,128)(2,1)S(1)}, u32[]{:S(2)}, u32[]{:S(2)}) collective-permute-start(bf16[2,2,4,128,128]{4,3,2,1,0:T(8,128)(2,1)S(1)} %all_to_all.5.refs_3_), channel_id=1, source_target_pairs={{0,2},{4,6},{8,10},{12,14},{16,18},{20,22},{24,26},{28,30},{1,3},{... | collective-permute-start | bytes 1572872 | tf_op jit(solution)/shard_map/ppermute | solution.py:140
  15.6 3.5 %collective-permute-start.9 = (bf16[2,2,4,128,128]{4,3,2,1,0:T(8,128)(2,1)S(1)}, bf16[2,2,4,128,128]{4,3,2,1,0:T(8,128)(2,1)S(1)}, u32[]{:S(2)}, u32[]{:S(2)}) collective-permute-start(bf16[2,2,4,128,128]{4,3,2,1,0:T(8,128)(2,1)S(1)} %all_to_all.5.refs_3_), channel_id=1, source_target_pairs={{0,4},{2,6},{8,12},{10,14},{16,20},{18,22},{24,28},{26,30},{1,5},{... | collective-permute-start | bytes 1572872 | tf_op jit(solution)/shard_map/ppermute | solution.py:140
  19.9 0.1 stack.80
  20.0 0.2 compare_reduce_fusion
  20.2 2.6 %collective-permute-done.refs_4_ = bf16[2,2,4,128,128]{4,3,2,1,0:T(8,128)(2,1)} collective-permute-done((bf16[2,2,4,128,128]{4,3,2,1,0:T(8,128)(2,1)S(1)}, bf16[2,2,4,128,128]{4,3,2,1,0:T(8,128)(2,1)}, u32[]{:S(2)}, u32[]{:S(2)}) %collective-permute-start) | collective-permute-done | bytes 524320 | tf_op jit(solution)/shard_map/ppermute | solution.py:140
  22.8 4.5 %collective-permute-start.4 = (bf16[2,2,4,128,128]{4,3,2,1,0:T(8,128)(2,1)}, bf16[2,2,4,128,128]{4,3,2,1,0:T(8,128)(2,1)S(1)}, u32[]{:S(2)}, u32[]{:S(2)}) collective-permute-start(bf16[2,2,4,128,128]{4,3,2,1,0:T(8,128)(2,1)} %collective-permute-done.refs_4_), channel_id=1, source_target_pairs={{0,8},{2,10},{4,12},{6,14},{8,16},{10,18},{12,20},{14,22},{16,24},... | collective-permute-start | bytes 1572872 | tf_op jit(solution)/shard_map/ppermute | solution.py:140
  27.3 1.6 %collective-permute-start.1 = (bf16[2,2,4,128,128]{4,3,2,1,0:T(8,128)(2,1)}, bf16[2,2,4,128,128]{4,3,2,1,0:T(8,128)(2,1)S(1)}, u32[]{:S(2)}, u32[]{:S(2)}) collective-permute-start(bf16[2,2,4,128,128]{4,3,2,1,0:T(8,128)(2,1)} %collective-permute-done.refs_4_), channel_id=1, source_target_pairs={{0,2},{2,0},{4,6},{6,4},{8,10},{10,8},{12,14},{14,12},{16,18},{18,... | collective-permute-start | bytes 1572872 | tf_op jit(solution)/shard_map/ppermute | solution.py:140
  28.9 1.5 %collective-permute-start.2 = (bf16[2,2,4,128,128]{4,3,2,1,0:T(8,128)(2,1)}, bf16[2,2,4,128,128]{4,3,2,1,0:T(8,128)(2,1)S(1)}, u32[]{:S(2)}, u32[]{:S(2)}) collective-permute-start(bf16[2,2,4,128,128]{4,3,2,1,0:T(8,128)(2,1)} %collective-permute-done.refs_4_), channel_id=1, source_target_pairs={{0,4},{2,6},{4,0},{6,2},{8,12},{10,14},{12,8},{14,10},{16,20},{18,... | collective-permute-start | bytes 1572872 | tf_op jit(solution)/shard_map/ppermute | solution.py:140
  30.4 7.8 %collective-permute-done.4.refs_3_ = bf16[2,2,4,128,128]{4,3,2,1,0:T(8,128)(2,1)S(1)} collective-permute-done((bf16[2,2,4,128,128]{4,3,2,1,0:T(8,128)(2,1)}, bf16[2,2,4,128,128]{4,3,2,1,0:T(8,128)(2,1)S(1)}, u32[]{:S(2)}, u32[]{:S(2)}) %collective-permute-start.4) | collective-permute-done | bytes 524320 | tf_op jit(solution)/shard_map/ppermute | solution.py:140
  38.2 1.3 %collective-permute-start.5 = (bf16[2,2,4,128,128]{4,3,2,1,0:T(8,128)(2,1)S(1)}, bf16[2,2,4,128,128]{4,3,2,1,0:T(8,128)(2,1)S(1)}, u32[]{:S(2)}, u32[]{:S(2)}) collective-permute-start(bf16[2,2,4,128,128]{4,3,2,1,0:T(8,128)(2,1)S(1)} %collective-permute-done.4.refs_3_), channel_id=1, source_target_pairs={{4,0},{6,2},{12,8},{14,10},{20,16},{22,18},{28,24},{30,26},{5,1},{... | collective-permute-start | bytes 1572872 | tf_op jit(solution)/shard_map/ppermute | solution.py:140
  39.5 1.3 %collective-permute-start.6 = (bf16[2,2,4,128,128]{4,3,2,1,0:T(8,128)(2,1)S(1)}, bf16[2,2,4,128,128]{4,3,2,1,0:T(8,128)(2,1)S(1)}, u32[]{:S(2)}, u32[]{:S(2)}) collective-permute-start(bf16[2,2,4,128,128]{4,3,2,1,0:T(8,128)(2,1)S(1)} %collective-permute-done.4.refs_3_), channel_id=1, source_target_pairs={{2,0},{6,4},{10,8},{14,12},{18,16},{22,20},{26,24},{30,28},{3,1},{... | collective-permute-start | bytes 1572872 | tf_op jit(solution)/shard_map/ppermute | solution.py:140
  40.8 1.0 broadcast_select_fusion
  41.9 1.5 %collective-permute-start.10 = (bf16[2,2,4,128,128]{4,3,2,1,0:T(8,128)(2,1)}, bf16[2,2,4,128,128]{4,3,2,1,0:T(8,128)(2,1)}, u32[]{:S(2)}, u32[]{:S(2)}) collective-permute-start(bf16[2,2,4,128,128]{4,3,2,1,0:T(8,128)(2,1)} %broadcast_select_fusion), channel_id=1, source_target_pairs={{2,6},{6,4},{10,14},{14,12},{18,22},{22,20},{26,30},{30,28},{3,7},... | collective-permute-start | bytes 1572872 | tf_op jit(solution)/shard_map/ppermute | solution.py:140
  43.3 0.9 broadcast_select_fusion.2
  44.3 2.6 %collective-permute-start.3 = (bf16[2,2,4,128,128]{4,3,2,1,0:T(8,128)(2,1)}, bf16[2,2,4,128,128]{4,3,2,1,0:T(8,128)(2,1)S(1)}, u32[]{:S(2)}, u32[]{:S(2)}) collective-permute-start(bf16[2,2,4,128,128]{4,3,2,1,0:T(8,128)(2,1)} %broadcast_select_fusion.2), channel_id=1, source_target_pairs={{0,4},{2,0},{4,6},{6,2},{8,12},{10,8},{12,14},{14,10},{16,20},{18,... | collective-permute-start | bytes 1572872 | tf_op jit(solution)/shard_map/ppermute | solution.py:140
  46.8 6.0 %collective-permute-done.5.refs_8_ = bf16[2,2,4,128,128]{4,3,2,1,0:T(8,128)(2,1)S(1)} collective-permute-done((bf16[2,2,4,128,128]{4,3,2,1,0:T(8,128)(2,1)S(1)}, bf16[2,2,4,128,128]{4,3,2,1,0:T(8,128)(2,1)S(1)}, u32[]{:S(2)}, u32[]{:S(2)}) %collective-permute-start.5) | collective-permute-done | bytes 524320 | tf_op jit(solution)/shard_map/ppermute | solution.py:140
  52.9 3.3 %collective-permute-done.6.refs_7_ = bf16[2,2,4,128,128]{4,3,2,1,0:T(8,128)(2,1)S(1)} collective-permute-done((bf16[2,2,4,128,128]{4,3,2,1,0:T(8,128)(2,1)S(1)}, bf16[2,2,4,128,128]{4,3,2,1,0:T(8,128)(2,1)S(1)}, u32[]{:S(2)}, u32[]{:S(2)}) %collective-permute-start.6) | collective-permute-done | bytes 524320 | tf_op jit(solution)/shard_map/ppermute | solution.py:140
  56.2 0.9 broadcast_select_fusion.1
  57.1 2.1 %collective-permute-start.7 = (bf16[2,2,4,128,128]{4,3,2,1,0:T(8,128)(2,1)}, bf16[2,2,4,128,128]{4,3,2,1,0:T(8,128)(2,1)S(1)}, u32[]{:S(2)}, u32[]{:S(2)}) collective-permute-start(bf16[2,2,4,128,128]{4,3,2,1,0:T(8,128)(2,1)} %broadcast_select_fusion.1), channel_id=1, source_target_pairs={{0,2},{4,0},{8,10},{12,8},{16,18},{20,16},{24,26},{28,24},{1,3},{5... | collective-permute-start | bytes 1572872 | tf_op jit(solution)/shard_map/ppermute | solution.py:140
  59.3 0.6 iota_add_fusion.refs_2_
  59.9 0.7 copy.23.meta
  60.6 1.2 %copy.26 = bf16[256,16,128]{2,0,1:T(8,128)(2,1)} copy(bf16[256,16,128]{2,1,0:T(8,128)(2,1)S(1)} %copy-done) | data formatting | bytes 2097152 | tf_op args[0]
  61.9 12.2 %shard_map.64 = (f32[4,4,256]{2,1,0:T(4,128)}, f32[4,4,8,256]{3,2,1,0:T(8,128)}, f32[16,128,256]{2,1,0:T(8,128)}) custom-call(s32[12,3]{1,0:T(8,128)} %copy.23.meta, bf16[16,256,128]{2,1,0:T(8,128)(2,1)} %bitcast.37, s32[1,256]{1,0:T(1,128)} %bitcast.45, s32[1,256]{1,0:T(1,128)} %iota_add_fusion.refs_2_, bf16[2,2,4,128,128]{4,3,2,1,0:T(8,128)(2,1)} %copy-done.3, ...), custom_call_target="tpu_custom_call" | custom-call | flops 2147483648 | tf_op jit(solution)/shard_map/pallas_call | solution.py:136
  74.1 17.4 %shard_map.65 = (f32[4,4,256]{2,1,0:T(4,128)}, f32[4,4,8,256]{3,2,1,0:T(8,128)}, f32[16,128,256]{2,1,0:T(8,128)}) custom-call(s32[12,3]{1,0:T(8,128)} %copy.23.meta, bf16[16,256,128]{2,1,0:T(8,128)(2,1)} %bitcast.38, s32[1,256]{1,0:T(1,128)} %bitcast.46, s32[1,256]{1,0:T(1,128)} %iota_add_fusion.refs_2_, bf16[2,2,4,128,128]{4,3,2,1,0:T(8,128)(2,1)} %copy-done.10, ...), custom_call_target="tpu_custom_call" | custom-call | flops 3221225472 | tf_op jit(solution)/shard_map/pallas_call | solution.py:136
  91.6 0.8 copy-done.1
  92.3 0.2 copy-done.2
  92.5 9.8 %shard_map.66 = bf16[16,256,128]{2,1,0:T(8,128)(2,1)} custom-call(s32[12,3]{1,0:T(8,128)} %copy.23.meta, bf16[16,256,128]{2,1,0:T(8,128)(2,1)} %bitcast.39, s32[1,256]{1,0:T(1,128)} %bitcast.47, s32[1,256]{1,0:T(1,128)} %iota_add_fusion.refs_2_, bf16[2,2,4,128,128]{4,3,2,1,0:T(8,128)(2,1)} %copy-done.1, bf16[2,2,4,128,128]{4,3,2,1,0:T(8,128)(2,1)} %copy-done.2, ...), custom_call_target="tpu_custom_call" | custom-call | flops 1073741824 | tf_op jit(solution)/shard_map/pallas_call | solution.py:136
  102.3 2.9 %copy.24 = bf16[256,16,128]{2,1,0:T(8,128)(2,1)} copy(bf16[256,16,128]{2,0,1:T(8,128)(2,1)} %bitcast.40) | data formatting | bytes 2097152 | tf_op jit(solution)/shard_map/transpose | solution.py:224
  (38 shorter events, 0.2 us)
Async XLA Ops:
  0.0 20.0 %copy-start.11 = (s32[1,18]{1,0:T(1,128)S(1)}, s32[1,18]{1,0:T(1,128)}, u32[]{:S(2)}) copy-start(s32[1,18]{1,0:T(1,128)} %param.10) | copy-start | bytes 220
  6.4 50.8 %copy-start.3 = (bf16[2,2,4,128,128]{4,3,2,1,0:T(8,128)(2,1)}, bf16[2,2,4,128,128]{4,3,2,1,0:T(8,128)(2,1)S(1)}, u32[]{:S(2)}) copy-start(bf16[2,2,4,128,128]{4,3,2,1,0:T(8,128)(2,1)S(1)} %all_to_all.5.refs_3_) | copy-start | bytes 1572868
  6.4 16.4 %collective-permute-start = (bf16[2,2,4,128,128]{4,3,2,1,0:T(8,128)(2,1)S(1)}, bf16[2,2,4,128,128]{4,3,2,1,0:T(8,128)(2,1)}, u32[]{:S(2)}, u32[]{:S(2)}) collective-permute-start(bf16[2,2,4,128,128]{4,3,2,1,0:T(8,128)(2,1)S(1)} %all_to_all.5.refs_3_), channel_id=1, source_target_pairs={{0,8},{2,10},{4,12},{6,14},{8,16},{10,18},{12,20},{14,22},{16,24},... | collective-permute-start | bytes 1572872 | tf_op jit(solution)/shard_map/ppermute | solution.py:140
  12.1 27.4 %collective-permute-start.8 = (bf16[2,2,4,128,128]{4,3,2,1,0:T(8,128)(2,1)S(1)}, bf16[2,2,4,128,128]{4,3,2,1,0:T(8,128)(2,1)S(1)}, u32[]{:S(2)}, u32[]{:S(2)}) collective-permute-start(bf16[2,2,4,128,128]{4,3,2,1,0:T(8,128)(2,1)S(1)} %all_to_all.5.refs_3_), channel_id=1, source_target_pairs={{0,2},{4,6},{8,10},{12,14},{16,18},{20,22},{24,26},{28,30},{1,3},{... | collective-permute-start | bytes 1572872 | tf_op jit(solution)/shard_map/ppermute | solution.py:140
  15.6 25.3 %collective-permute-start.9 = (bf16[2,2,4,128,128]{4,3,2,1,0:T(8,128)(2,1)S(1)}, bf16[2,2,4,128,128]{4,3,2,1,0:T(8,128)(2,1)S(1)}, u32[]{:S(2)}, u32[]{:S(2)}) collective-permute-start(bf16[2,2,4,128,128]{4,3,2,1,0:T(8,128)(2,1)S(1)} %all_to_all.5.refs_3_), channel_id=1, source_target_pairs={{0,4},{2,6},{8,12},{10,14},{16,20},{18,22},{24,28},{26,30},{1,5},{... | collective-permute-start | bytes 1572872 | tf_op jit(solution)/shard_map/ppermute | solution.py:140
  22.8 15.4 %collective-permute-start.4 = (bf16[2,2,4,128,128]{4,3,2,1,0:T(8,128)(2,1)}, bf16[2,2,4,128,128]{4,3,2,1,0:T(8,128)(2,1)S(1)}, u32[]{:S(2)}, u32[]{:S(2)}) collective-permute-start(bf16[2,2,4,128,128]{4,3,2,1,0:T(8,128)(2,1)} %collective-permute-done.refs_4_), channel_id=1, source_target_pairs={{0,8},{2,10},{4,12},{6,14},{8,16},{10,18},{12,20},{14,22},{16,24},... | collective-permute-start | bytes 1572872 | tf_op jit(solution)/shard_map/ppermute | solution.py:140
  27.3 16.0 %collective-permute-start.1 = (bf16[2,2,4,128,128]{4,3,2,1,0:T(8,128)(2,1)}, bf16[2,2,4,128,128]{4,3,2,1,0:T(8,128)(2,1)S(1)}, u32[]{:S(2)}, u32[]{:S(2)}) collective-permute-start(bf16[2,2,4,128,128]{4,3,2,1,0:T(8,128)(2,1)} %collective-permute-done.refs_4_), channel_id=1, source_target_pairs={{0,2},{2,0},{4,6},{6,4},{8,10},{10,8},{12,14},{14,12},{16,18},{18,... | collective-permute-start | bytes 1572872 | tf_op jit(solution)/shard_map/ppermute | solution.py:140
  28.9 14.4 %collective-permute-start.2 = (bf16[2,2,4,128,128]{4,3,2,1,0:T(8,128)(2,1)}, bf16[2,2,4,128,128]{4,3,2,1,0:T(8,128)(2,1)S(1)}, u32[]{:S(2)}, u32[]{:S(2)}) collective-permute-start(bf16[2,2,4,128,128]{4,3,2,1,0:T(8,128)(2,1)} %collective-permute-done.refs_4_), channel_id=1, source_target_pairs={{0,4},{2,6},{4,0},{6,2},{8,12},{10,14},{12,8},{14,10},{16,20},{18,... | collective-permute-start | bytes 1572872 | tf_op jit(solution)/shard_map/ppermute | solution.py:140
  30.4 30.2 %copy-start = (bf16[256,16,128]{2,1,0:T(8,128)(2,1)S(1)}, bf16[256,16,128]{2,1,0:T(8,128)(2,1)}, u32[]{:S(2)}) copy-start(bf16[256,16,128]{2,1,0:T(8,128)(2,1)} %param.6) | copy-start | bytes 3145732
  38.2 21.1 %copy-start.10 = (bf16[2,2,4,128,128]{4,3,2,1,0:T(8,128)(2,1)}, bf16[2,2,4,128,128]{4,3,2,1,0:T(8,128)(2,1)S(1)}, u32[]{:S(2)}) copy-start(bf16[2,2,4,128,128]{4,3,2,1,0:T(8,128)(2,1)S(1)} %collective-permute-done.4.refs_3_) | copy-start | bytes 1572868
  38.2 14.7 %collective-permute-start.5 = (bf16[2,2,4,128,128]{4,3,2,1,0:T(8,128)(2,1)S(1)}, bf16[2,2,4,128,128]{4,3,2,1,0:T(8,128)(2,1)S(1)}, u32[]{:S(2)}, u32[]{:S(2)}) collective-permute-start(bf16[2,2,4,128,128]{4,3,2,1,0:T(8,128)(2,1)S(1)} %collective-permute-done.4.refs_3_), channel_id=1, source_target_pairs={{4,0},{6,2},{12,8},{14,10},{20,16},{22,18},{28,24},{30,26},{5,1},{... | collective-permute-start | bytes 1572872 | tf_op jit(solution)/shard_map/ppermute | solution.py:140
  39.5 17.6 %copy-start.4 = (bf16[2,2,4,128,128]{4,3,2,1,0:T(8,128)(2,1)}, bf16[2,2,4,128,128]{4,3,2,1,0:T(8,128)(2,1)S(1)}, u32[]{:S(2)}) copy-start(bf16[2,2,4,128,128]{4,3,2,1,0:T(8,128)(2,1)S(1)} %collective-permute-done.8.refs_5_) | copy-start | bytes 1572868
  39.5 16.7 %collective-permute-start.6 = (bf16[2,2,4,128,128]{4,3,2,1,0:T(8,128)(2,1)S(1)}, bf16[2,2,4,128,128]{4,3,2,1,0:T(8,128)(2,1)S(1)}, u32[]{:S(2)}, u32[]{:S(2)}) collective-permute-start(bf16[2,2,4,128,128]{4,3,2,1,0:T(8,128)(2,1)S(1)} %collective-permute-done.4.refs_3_), channel_id=1, source_target_pairs={{2,0},{6,4},{10,8},{14,12},{18,16},{22,20},{26,24},{30,28},{3,1},{... | collective-permute-start | bytes 1572872 | tf_op jit(solution)/shard_map/ppermute | solution.py:140
  40.8 2.5 %copy-start.5 = (bf16[2,2,4,128,128]{4,3,2,1,0:T(8,128)(2,1)}, bf16[2,2,4,128,128]{4,3,2,1,0:T(8,128)(2,1)S(1)}, u32[]{:S(2)}) copy-start(bf16[2,2,4,128,128]{4,3,2,1,0:T(8,128)(2,1)S(1)} %collective-permute-done.9.refs_6_) | copy-start | bytes 1572868
  41.9 32.2 %collective-permute-start.10 = (bf16[2,2,4,128,128]{4,3,2,1,0:T(8,128)(2,1)}, bf16[2,2,4,128,128]{4,3,2,1,0:T(8,128)(2,1)}, u32[]{:S(2)}, u32[]{:S(2)}) collective-permute-start(bf16[2,2,4,128,128]{4,3,2,1,0:T(8,128)(2,1)} %broadcast_select_fusion), channel_id=1, source_target_pairs={{2,6},{6,4},{10,14},{14,12},{18,22},{22,20},{26,30},{30,28},{3,7},... | collective-permute-start | bytes 1572872 | tf_op jit(solution)/shard_map/ppermute | solution.py:140
  43.3 12.9 %copy-start.6 = (bf16[2,2,4,128,128]{4,3,2,1,0:T(8,128)(2,1)}, bf16[2,2,4,128,128]{4,3,2,1,0:T(8,128)(2,1)S(1)}, u32[]{:S(2)}) copy-start(bf16[2,2,4,128,128]{4,3,2,1,0:T(8,128)(2,1)S(1)} %collective-permute-done.1.refs_4_) | copy-start | bytes 1572868
  43.3 16.0 %copy-start.7 = (bf16[2,2,4,128,128]{4,3,2,1,0:T(8,128)(2,1)}, bf16[2,2,4,128,128]{4,3,2,1,0:T(8,128)(2,1)S(1)}, u32[]{:S(2)}) copy-start(bf16[2,2,4,128,128]{4,3,2,1,0:T(8,128)(2,1)S(1)} %collective-permute-done.2.refs_5_) | copy-start | bytes 1572868
  44.3 47.3 %collective-permute-start.3 = (bf16[2,2,4,128,128]{4,3,2,1,0:T(8,128)(2,1)}, bf16[2,2,4,128,128]{4,3,2,1,0:T(8,128)(2,1)S(1)}, u32[]{:S(2)}, u32[]{:S(2)}) collective-permute-start(bf16[2,2,4,128,128]{4,3,2,1,0:T(8,128)(2,1)} %broadcast_select_fusion.2), channel_id=1, source_target_pairs={{0,4},{2,0},{4,6},{6,2},{8,12},{10,8},{12,14},{14,10},{16,20},{18,... | collective-permute-start | bytes 1572872 | tf_op jit(solution)/shard_map/ppermute | solution.py:140
  52.9 6.4 %copy-start.8 = (bf16[2,2,4,128,128]{4,3,2,1,0:T(8,128)(2,1)}, bf16[2,2,4,128,128]{4,3,2,1,0:T(8,128)(2,1)S(1)}, u32[]{:S(2)}) copy-start(bf16[2,2,4,128,128]{4,3,2,1,0:T(8,128)(2,1)S(1)} %collective-permute-done.5.refs_8_) | copy-start | bytes 1572868
  56.2 3.1 %copy-start.9 = (bf16[2,2,4,128,128]{4,3,2,1,0:T(8,128)(2,1)}, bf16[2,2,4,128,128]{4,3,2,1,0:T(8,128)(2,1)S(1)}, u32[]{:S(2)}) copy-start(bf16[2,2,4,128,128]{4,3,2,1,0:T(8,128)(2,1)S(1)} %collective-permute-done.6.refs_7_) | copy-start | bytes 1572868
  57.1 34.4 %collective-permute-start.7 = (bf16[2,2,4,128,128]{4,3,2,1,0:T(8,128)(2,1)}, bf16[2,2,4,128,128]{4,3,2,1,0:T(8,128)(2,1)S(1)}, u32[]{:S(2)}, u32[]{:S(2)}) collective-permute-start(bf16[2,2,4,128,128]{4,3,2,1,0:T(8,128)(2,1)} %broadcast_select_fusion.1), channel_id=1, source_target_pairs={{0,2},{4,0},{8,10},{12,8},{16,18},{20,16},{24,26},{28,24},{1,3},{5... | collective-permute-start | bytes 1572872 | tf_op jit(solution)/shard_map/ppermute | solution.py:140
  91.5 0.8 copy-start.1
  91.6 1.0 copy-start.2
